TPU v7x, 32 devices: a whole 2x2x4 slice. The times are simulated.
32 devices in a mesh: rows: 8 (over z, x), cols: 4 (over y, core).
Axes of the slice: x: 2, y: 2, z: 4, core: 2. Of those that a mesh axis runs over, the one named last changes fastest.
Arguments:
- basis: bfloat16 [65536, 512], P('rows', 'cols'), may hold values from -6 to 6
- lower: bfloat16 [256, 256, 256], P('rows'), may hold values from -0.375 to 0.375
- diag: bfloat16 [256, 256, 256], P('rows'), may hold values from -0.375 to 0.375
- upper: bfloat16 [256, 256, 256], P('rows'), may hold values from -0.375 to 0.375
- inverse: bfloat16 [256, 256, 256], P('rows'), may hold values from -0.375 to 0.375
Outputs:
- ortho: bfloat16 [65536, 512], P('rows', 'cols')
- projected: float32 [512, 512], P(None, 'cols')
All inputs are finite; a program needn't handle non-finite values.
Results may differ from a plain program's by a relative error of at most 0.0085.
Values may be sent and summed in bfloat16 or wider, within the bound.
A program may use at most 128 MiB of HBM per device.

v0:
```python
import jax
import jax.numpy as jnp
from jax import lax
from jax.sharding import PartitionSpec as P


def extended(block, sides, width):
    for axis, dim in sides:
        count = lax.axis_size(axis)
        forward = [(i, i + 1) for i in range(count - 1)]
        backward = [(target, source) for source, target in forward]
        low = lax.ppermute(
            lax.slice_in_dim(block, block.shape[dim] - width, None, axis=dim), axis, forward
        )
        high = lax.ppermute(lax.slice_in_dim(block, 0, width, axis=dim), axis, backward)
        block = jnp.concatenate([low, block, high], axis=dim)
    return block


def inner(left, right):
    return lax.dot_general(
        left, right, (((0,), (0,)), ((), ())), preferred_element_type=jnp.float32
    )


def apply_blocks(padded, lower, diag, upper, inverse):
    count = diag.shape[0]
    size = diag.shape[1]
    width = padded.shape[1]
    blocks = padded.reshape(count + 2, size, width)
    mixed = jnp.einsum("bij,bjc->bic", lower, blocks[:-2], preferred_element_type=jnp.float32)
    mixed = mixed + jnp.einsum(
        "bij,bjc->bic", diag, blocks[1:-1], preferred_element_type=jnp.float32
    )
    mixed = mixed + jnp.einsum(
        "bij,bjc->bic", upper, blocks[2:], preferred_element_type=jnp.float32
    )
    mixed = mixed.astype(jnp.bfloat16)
    result = jnp.einsum("bij,bjc->bic", inverse, mixed, preferred_element_type=jnp.float32)
    return result.astype(jnp.bfloat16).reshape(count * size, width)


def inverse_upper(gram):
    factor = jnp.linalg.cholesky(gram)
    identity = jnp.eye(gram.shape[0], dtype=jnp.float32)
    linv = lax.linalg.triangular_solve(factor, identity, left_side=True, lower=True)
    return linv.T.astype(jnp.bfloat16)


def shards(basis, lower, diag, upper, inverse):
    size = diag.shape[1]
    width = basis.shape[1]

    def operate(field):
        padded = extended(field, (("rows", 0),), size)
        return apply_blocks(padded, lower, diag, upper, inverse)

    work = operate(basis)
    wide = lax.all_gather(work, "cols", axis=1, tiled=True)
    gram = lax.psum(inner(wide, wide), "rows")
    rinv = inverse_upper(gram)
    start = lax.axis_index("cols") * width
    ortho_all = jnp.dot(wide, rinv, preferred_element_type=jnp.float32).astype(jnp.bfloat16)
    ortho = lax.dynamic_slice_in_dim(ortho_all, start, width, 1)
    image = operate(ortho)
    projected = lax.psum(inner(ortho_all, image), "rows")
    return (ortho, projected)


def solution(mesh):
    in_specs = (
        P("rows", "cols"),
        P("rows", None, None),
        P("rows", None, None),
        P("rows", None, None),
        P("rows", None, None),
    )
    out_specs = (P("rows", "cols"), P(None, "cols"))
    return jax.shard_map(shards, mesh=mesh, in_specs=in_specs, out_specs=out_specs, check_vma=False)
```

profile of v0, /device:TPU:0, one launch (start us, length us, event | category | flops | bytes accessed | tf_op | source)
XLA Modules:
  0.0 457.5 jit_solution(3944854083608453380)
XLA Ops:
  9.4 5.5 %collective-permute-start = (bf16[256,128]{1,0:T(8,128)(2,1)S(1)}, bf16[256,128]{1,0:T(8,128)(2,1)S(1)}, u32[]{:S(2)}, u32[]{:S(2)}) collective-permute-start(bf16[256,128]{1,0:T(8,128)(2,1)S(1)} %get-tuple-element.27), channel_id=1, source_target_pairs={{0,4},{4,8},{8,12},{12,16},{16,20},{20,24},{24,28},{1,5},{5,9},{9,... | collective-permute-start | bytes 196616 | tf_op jit(solution)/shard_map/ppermute | solution.py:12
  14.9 6.5 %fusion.49 = f32[32,256,128]{1,2,0:T(8,128)} fusion(bf16[32,256,256]{2,1,0:T(8,128)(2,1)} %param.7, bf16[32,256,128]{2,1,0:T(8,128)(2,1)} %bitcast.98), kind=kOutput, calls=%fused_computation.97 | convolution fusion | flops 536870912 | bytes 10485760 | tf_op jit(solution)/shard_map/bij,bjc->bic/dot_general | solution.py:32
  23.6 3.5 fusion.48
  27.0 10.1 %convert_bitcast_fusion.1 = bf16[32,256,128]{1,2,0:T(8,128)(2,1)} fusion(bf16[32,256,256]{2,1,0:T(8,128)(2,1)} %param.9, f32[32,256,128]{1,2,0:T(8,128)} %fusion.49, f32[32,128,256]{2,1,0:T(8,128)} %fusion.48, bf16[32,256,128]{2,1,0:T(8,128)(2,1)S(1)} %bitcast.99, bf16[32,256,256]{2,1,0:T(8,128)(2,1)} %param.8), kind=kOutput, calls=%fused_computation.14 | convolution fusion | flops 1077936128 | bytes 20971520 | tf_op jit(solution)/shard_map/bij,bjc->bic/dot_general | solution.py:39
  37.1 4.0 copy.9
  41.2 61.1 %all-gather.2.cloned.1.call-done = bf16[8192,512]{1,0:T(8,128)(2,1)} async-done(((bf16[8192,128]{1,0:T(8,128)(2,1)}), bf16[8192,512]{1,0:T(8,128)(2,1)}) %all-gather.2.cloned.1.call-update) | async-done | bytes 8388624 | tf_op jit(solution)/shard_map/all_gather | solution.py:59
  102.4 11.3 %fusion.50 = f32[512,512]{0,1:T(8,128)} fusion(bf16[8192,512]{1,0:T(8,128)(2,1)} %all-gather.2.cloned.1.call-done), kind=kOutput, calls=%fused_computation.98 | convolution fusion | flops 4294967296 | bytes 9437184 | tf_op jit(solution)/shard_map/dot_general | solution.py:21
  114.8 77.2 %all-reduce.4.cloned.1.call-done = f32[512,512]{0,1:T(8,128)} async-done(((f32[512,512]{0,1:T(8,128)}), f32[512,512]{0,1:T(8,128)}) %all-reduce.4.cloned.1.call-update) | async-done | bytes 1048592 | tf_op jit(solution)/shard_map/psum | solution.py:60
  195.1 11.7 %cholesky.104 = f32[128,128]{1,0:T(8,128)S(1)} custom-call(f32[128,128]{1,0:T(8,128)S(1)} %cholesky.266), custom_call_target="Cholesky" | custom-call | tf_op jit(solution)/shard_map/jit(cholesky)/cholesky | solution.py:44
  206.8 9.8 %custom-call.30 = f32[1,128,128]{1,2,0:T(8,128)S(1)} custom-call(f32[1,128,128]{2,1,0:T(8,128)S(1)} %get-tuple-element.37), custom_call_target="InvertDiagBlocksLowerTriangular" | custom-call | tf_op jit(solution)/shard_map/jit(cholesky)/cholesky | solution.py:44
  217.4 11.7 %cholesky.217 = f32[128,128]{1,0:T(8,128)S(1)} custom-call(f32[128,128]{1,0:T(8,128)S(1)} %cholesky.270), custom_call_target="Cholesky" | custom-call | tf_op jit(solution)/shard_map/jit(cholesky)/cholesky | solution.py:44
  229.2 10.0 %custom-call.31 = f32[1,128,128]{1,2,0:T(8,128)S(1)} custom-call(f32[1,128,128]{2,1,0:T(8,128)S(1)} %get-tuple-element.34), custom_call_target="InvertDiagBlocksLowerTriangular" | custom-call | tf_op jit(solution)/shard_map/jit(cholesky)/cholesky | solution.py:44
  239.8 11.7 %cholesky.238 = f32[128,128]{1,0:T(8,128)S(1)} custom-call(f32[128,128]{1,0:T(8,128)S(1)} %cholesky.275), custom_call_target="Cholesky" | custom-call | tf_op jit(solution)/shard_map/jit(cholesky)/cholesky | solution.py:44
  252.3 9.8 %custom-call.32 = f32[1,128,128]{1,2,0:T(8,128)S(1)} custom-call(f32[1,128,128]{2,1,0:T(8,128)S(1)} %get-tuple-element.31), custom_call_target="InvertDiagBlocksLowerTriangular" | custom-call | tf_op jit(solution)/shard_map/jit(cholesky)/cholesky | solution.py:44
  262.7 11.7 %cholesky.255 = f32[128,128]{1,0:T(8,128)S(1)} custom-call(f32[128,128]{1,0:T(8,128)S(1)} %convolution_subtract_fusion.5), custom_call_target="Cholesky" | custom-call | tf_op jit(solution)/shard_map/jit(cholesky)/cholesky | solution.py:44
  278.9 10.8 %while.1 = (s32[]{:T(128)}, f32[512,512]{1,0:T(8,128)S(1)}, s32[4,2]{0,1:T(2,128)S(1)}, f32[4,128,128]{2,1,0:T(8,128)}, s32[]{:T(128)}) while((s32[]{:T(128)}, f32[512,512]{1,0:T(8,128)S(1)}, s32[4,2]{0,1:T(2,128)S(1)}, f32[4,128,128]{2,1,0:T(8,128)}, s32[]{:T(128)}) %tuple.38), condition=%wide.while_cond, body=%wide.while_body.sunk | while | flops 2 | bytes 132205 | solution.py:46
  289.7 40.1 %custom-call.33 = f32[4,128,128]{1,2,0:T(8,128)S(1)} custom-call(f32[4,128,128]{2,1,0:T(8,128)} %get-tuple-element.9), custom_call_target="InvertDiagBlocksLowerTriangular" | custom-call | tf_op jit(solution)/shard_map/triangular_solve | solution.py:46
  333.7 8.8 %convolution_convert_fusion = bf16[8192,512]{1,0:T(8,128)(2,1)S(1)} fusion(bf16[8192,512]{1,0:T(8,128)(2,1)} %all-gather.2.cloned.1.call-done, bf16[128,512]{1,0:T(8,128)(2,1)S(1)} %convolution_convert_fusion.1, bf16[128,512]{1,0:T(8,128)(2,1)S(1)} %get-tuple-element.40, bf16[128,512]{1,0:T(8,128)(2,1)S(1)} %get-tuple-element.42, ...), kind=kOutput, calls=%fused_computation.2 | convolution fusion | flops 4301258752 | bytes 17301504 | tf_op jit(solution)/shard_map/dot_general | solution.py:63
  342.9 3.6 collective-permute-start.2
  348.1 3.4 fusion.51
  353.7 3.5 fusion.52
  357.2 10.1 %convert_bitcast_fusion = bf16[32,256,128]{1,2,0:T(8,128)(2,1)} fusion(bf16[32,256,256]{2,1,0:T(8,128)(2,1)} %param.9, f32[32,128,256]{2,1,0:T(8,128)} %fusion.52, f32[32,128,256]{2,1,0:T(8,128)} %fusion.51, bf16[32,256,128]{2,1,0:T(8,128)(2,1)S(1)} %bitcast.100, bf16[32,256,256]{2,1,0:T(8,128)(2,1)} %param.6), kind=kOutput, calls=%fused_computation.13 | convolution fusion | flops 1077936128 | bytes 20971520 | tf_op jit(solution)/shard_map/bij,bjc->bic/dot_general | solution.py:39
  370.5 6.4 %fusion.53 = f32[512,128]{1,0:T(8,128)} fusion(bf16[8192,512]{1,0:T(8,128)(2,1)} %copy-done.5, bf16[8192,128]{1,0:T(8,128)(2,1)S(1)} %bitcast.104), kind=kOutput, calls=%fused_computation.101 | convolution fusion | flops 1073741824 | bytes 10747904 | tf_op jit(solution)/shard_map/dot_general | solution.py:21
  376.9 72.2 %all-reduce.6.cloned.1.call-done = f32[512,128]{1,0:T(8,128)} async-done(((f32[512,128]{1,0:T(8,128)}), f32[512,128]{1,0:T(8,128)}) %all-reduce.6.cloned.1.call-update) | async-done | bytes 262160 | tf_op jit(solution)/shard_map/psum | solution.py:66
  (75 shorter events, 36.9 us)
Async XLA Ops:
  7.2 95.2 %all-gather.2.cloned.1.call-start = ((), (), s32[]{:S(2)}) async-start(), calls=%async_computation | async-start | bytes 10485760 | tf_op jit(solution)/shard_map/all_gather | solution.py:59
  8.1 13.3 %collective-permute-start.1 = (bf16[256,128]{1,0:T(8,128)(2,1)S(1)}, bf16[256,128]{1,0:T(8,128)(2,1)S(1)}, u32[]{:S(2)}, u32[]{:S(2)}) collective-permute-start(bf16[256,128]{1,0:T(8,128)(2,1)S(1)} %get-tuple-element.26), channel_id=1, source_target_pairs={{4,0},{8,4},{12,8},{16,12},{20,16},{24,20},{28,24},{5,1},{9,5},{13... | collective-permute-start | bytes 196616 | tf_op jit(solution)/shard_map/ppermute | solution.py:15
  9.4 12.0 %collective-permute-start = (bf16[256,128]{1,0:T(8,128)(2,1)S(1)}, bf16[256,128]{1,0:T(8,128)(2,1)S(1)}, u32[]{:S(2)}, u32[]{:S(2)}) collective-permute-start(bf16[256,128]{1,0:T(8,128)(2,1)S(1)} %get-tuple-element.27), channel_id=1, source_target_pairs={{0,4},{4,8},{8,12},{12,16},{16,20},{20,24},{24,28},{1,5},{5,9},{9,... | collective-permute-start | bytes 196616 | tf_op jit(solution)/shard_map/ppermute | solution.py:12
  14.9 6.5 %copy-start.4 = (bf16[8192,128]{1,0:T(8,128)(2,1)S(1)}, bf16[8192,128]{1,0:T(8,128)(2,1)}, u32[]{:S(2)}) copy-start(bf16[8192,128]{1,0:T(8,128)(2,1)} %param.5) | copy-start | bytes 6291460
  21.4 2.2 copy-start.2
  41.2 150.9 %all-reduce.4.cloned.1.call-start = ((), (), s32[]{:S(2)}) async-start(), calls=%async_computation.1 | async-start | bytes 2097152 | tf_op jit(solution)/shard_map/psum | solution.py:60
  113.7 335.5 %all-reduce.6.cloned.1.call-start = ((), (), s32[]{:S(2)}) async-start(), calls=%async_computation.2 | async-start | bytes 524288 | tf_op jit(solution)/shard_map/psum | solution.py:66
  342.5 9.0 %copy-start.5 = (bf16[8192,512]{1,0:T(8,128)(2,1)}, bf16[8192,512]{1,0:T(8,128)(2,1)S(1)}, u32[]{:S(2)}) copy-start(bf16[8192,512]{1,0:T(8,128)(2,1)S(1)} %convolution_convert_fusion) | copy-start | bytes 25165828
  342.5 5.6 %copy-start.3 = (bf16[32,256,256]{2,1,0:T(8,128)(2,1)S(1)}, bf16[32,256,256]{2,1,0:T(8,128)(2,1)}, u32[]{:S(2)}) copy-start(bf16[32,256,256]{2,1,0:T(8,128)(2,1)} %param.7) | copy-start | bytes 12582916
  342.8 9.9 %copy-start = (bf16[8192,128]{1,0:T(8,128)(2,1)}, bf16[8192,128]{1,0:T(8,128)(2,1)S(1)}, u32[]{:S(2)}) copy-start(bf16[8192,128]{1,0:T(8,128)(2,1)S(1)} %constant_dynamic-slice_fusion.2) | copy-start | bytes 6291460
  342.9 8.7 %collective-permute-start.2 = (bf16[256,128]{1,0:T(8,128)(2,1)S(1)}, bf16[256,128]{1,0:T(8,128)(2,1)S(1)}, u32[]{:S(2)}, u32[]{:S(2)}) collective-permute-start(bf16[256,128]{1,0:T(8,128)(2,1)S(1)} %get-tuple-element.20), channel_id=1, source_target_pairs={{0,4},{4,8},{8,12},{12,16},{16,20},{20,24},{24,28},{1,5},{5,9},{9,... | collective-permute-start | bytes 196616 | tf_op jit(solution)/shard_map/ppermute | solution.py:12
  346.5 6.3 %collective-permute-start.3 = (bf16[256,128]{1,0:T(8,128)(2,1)S(1)}, bf16[256,128]{1,0:T(8,128)(2,1)S(1)}, u32[]{:S(2)}, u32[]{:S(2)}) collective-permute-start(bf16[256,128]{1,0:T(8,128)(2,1)S(1)} %get-tuple-element.21), channel_id=1, source_target_pairs={{4,0},{8,4},{12,8},{16,12},{20,16},{24,20},{28,24},{5,1},{9,5},{13... | collective-permute-start | bytes 196616 | tf_op jit(solution)/shard_map/ppermute | solution.py:15
  351.5 2.2 copy-start.1
Sparse Core Ops, SparseCore 0:
  41.3 61.0 all-gather.1
  113.8 78.2 all-reduce.3
  377.1 72.0 all-reduce.5
where the time goes:
time: 465 us; the launch traced here: 458 us
  waiting for transfers between devices  212 us (46%)
  other arithmetic  122 us (26%)
  matrix products  69.1 us (15%)
  local copies, waits for them, and re-layouts  25.2 us (5%)
  between operations  16.9 us (4%)
  starting transfers between devices  12.3 us (3%)
    another operation x14, other arithmetic, inverse_upper(): factor = jnp.linalg.cholesky(gram)  79 us
    psum x1, waiting for transfers between devices, shards(): gram = lax.psum(inner(wide, wide), 'rows')  77.2 us
    psum x1, waiting for transfers between devices, shards(): projected = lax.psum(inner(ortho_all, image), 'rows')  72.2 us
    all_gather x1, waiting for transfers between devices, shards(): wide = lax.all_gather(work, 'cols', axis=1, tiled=True)  61.1 us
    another operation x3, other arithmetic, inverse_upper(): lax.linalg.triangular_solve(factor, identity, left_side=True, lower=True)  40.3 us
    dot_general x2, matrix products, apply_blocks(): jnp.einsum('bij,bjc->bic', inverse, mixed, preferred_element_type=jnp.flo...  20.1 us
    dot_general x2, matrix products, inner(): lax.dot_general(left, right, (((0,), (0,)), ((), ())), preferred_element_...  17.7 us
    another operation x12, local copies, waits for them, and re-layouts  10.8 us
  transfers between devices with their start and end apart: 7, of which 4 were waited for; matrix products, arithmetic and copies ran while one was open for 2% of the time, Pallas kernels for 0%

commit v1 on v0

--- a/solution.py
+++ b/solution.py
@@ -1,7 +1,25 @@
+import functools
 import jax
 import jax.numpy as jnp
 from jax import lax
 from jax.sharding import PartitionSpec as P
+
+
+def balance_the_sides(u_in, device_axis, which_dim):
+    amount_of = lax.axis_size(device_axis)
+    inter = u_in
+    tray = [inter]
+    u1 = [(s - 1, s) for s in range(1, amount_of)] + [(amount_of - 1, 0)]
+    for _ in range(amount_of - 1):
+        inter = lax.ppermute(inter, device_axis, u1)
+        tray += [inter]
+    piece_out = jnp.concatenate([*reversed(tray)], axis=which_dim)
+    return jnp.roll(
+        piece_out, (lax.axis_index(device_axis) + 1) * inter.shape[which_dim], axis=which_dim
+    )
+
+
+_see_leaf = functools.partial(balance_the_sides, device_axis="cols", which_dim=1)
 
 
 def extended(block, sides, width):
@@ -56,7 +74,7 @@
         return apply_blocks(padded, lower, diag, upper, inverse)
 
     work = operate(basis)
-    wide = lax.all_gather(work, "cols", axis=1, tiled=True)
+    wide = _see_leaf(work)
     gram = lax.psum(inner(wide, wide), "rows")
     rinv = inverse_upper(gram)
     start = lax.axis_index("cols") * width

time: 465 us -> 503 us (1.082)
  local copies, waits for them, and re-layouts: 25.2 us -> 44.2 us
  waiting for transfers between devices: 212 us -> 229 us
    ppermute x0 -> x3, waiting for transfers between devices: none -> 76.8 us  [balance_the_sides(): inter = lax.ppermute(inter, device_axis, u1)]
    all_gather x1 -> x0, waiting for transfers between devices: 61.1 us -> none  [shards(): wide = lax.all_gather(work, 'cols', axis=1, tiled=True)]
    unnamed x13 -> x24, local copies, waits for them, and re-layouts: 4.26 us -> 23.2 us
  transfers between devices with their start and end apart: 7 -> 9, of which waited for: 4 -> 6; matrix products, arithmetic and copies ran while one was open for 2% -> 2% of each run, Pallas kernels for 0% -> 0%
where the time goes in v1:
time: 503 us; the launch traced here: 494 us
  waiting for transfers between devices  229 us (46%)
  other arithmetic  122 us (24%)
  matrix products  69.6 us (14%)
  local copies, waits for them, and re-layouts  44.2 us (9%)
  between operations  17 us (3%)
  starting transfers between devices  12.3 us (2%)
    psum x1, waiting for transfers between devices, shards(): gram = lax.psum(inner(wide, wide), 'rows')  79 us
    another operation x14, other arithmetic, inverse_upper(): factor = jnp.linalg.cholesky(gram)  79 us
    ppermute x3, waiting for transfers between devices, balance_the_sides(): inter = lax.ppermute(inter, device_axis, u1)  76.8 us
    psum x1, waiting for transfers between devices, shards(): projected = lax.psum(inner(ortho_all, image), 'rows')  72.2 us
    another operation x3, other arithmetic, inverse_upper(): lax.linalg.triangular_solve(factor, identity, left_side=True, lower=True)  40.3 us
    unnamed x24, local copies, waits for them, and re-layouts  23.2 us
    dot_general x2, matrix products, apply_blocks(): jnp.einsum('bij,bjc->bic', inverse, mixed, preferred_element_type=jnp.flo...  20.2 us
    dot_general x2, matrix products, inner(): lax.dot_general(left, right, (((0,), (0,)), ((), ())), preferred_element_...  18 us
  transfers between devices with their start and end apart: 9, of which 6 were waited for; matrix products, arithmetic and copies ran while one was open for 2% of the time, Pallas kernels for 0%

profile of v1, /device:TPU:0, one launch (start us, length us, event | category | flops | bytes accessed | tf_op | source)
XLA Modules:
  0.0 494.5 jit_solution(10446334319870662669)
XLA Ops:
  9.4 5.5 %collective-permute-start = (bf16[256,128]{1,0:T(8,128)(2,1)S(1)}, bf16[256,128]{1,0:T(8,128)(2,1)S(1)}, u32[]{:S(2)}, u32[]{:S(2)}) collective-permute-start(bf16[256,128]{1,0:T(8,128)(2,1)S(1)} %get-tuple-element.27), channel_id=1, source_target_pairs={{0,4},{4,8},{8,12},{12,16},{16,20},{20,24},{24,28},{1,5},{5,9},{9,... | collective-permute-start | bytes 196616 | tf_op jit(solution)/shard_map/ppermute | solution.py:30
  14.9 6.5 %fusion.54 = f32[32,256,128]{1,2,0:T(8,128)} fusion(bf16[32,256,256]{2,1,0:T(8,128)(2,1)} %param.7, bf16[32,256,128]{2,1,0:T(8,128)(2,1)} %bitcast.98), kind=kOutput, calls=%fused_computation.110 | convolution fusion | flops 536870912 | bytes 10485760 | tf_op jit(solution)/shard_map/bij,bjc->bic/dot_general | solution.py:50
  23.6 3.5 fusion.53
  27.1 10.1 %convert_bitcast_fusion.1 = bf16[32,256,128]{1,2,0:T(8,128)(2,1)} fusion(bf16[32,256,256]{2,1,0:T(8,128)(2,1)} %param.9, f32[32,256,128]{1,2,0:T(8,128)} %fusion.54, f32[32,128,256]{2,1,0:T(8,128)} %fusion.53, bf16[32,256,128]{2,1,0:T(8,128)(2,1)S(1)} %bitcast.99, bf16[32,256,256]{2,1,0:T(8,128)(2,1)} %param.8), kind=kOutput, calls=%fused_computation.17 | convolution fusion | flops 1077936128 | bytes 20971520 | tf_op jit(solution)/shard_map/bij,bjc->bic/dot_general | solution.py:57
  40.4 25.4 %collective-permute-done.2 = bf16[8192,128]{1,0:T(8,128)(2,1)S(1)} collective-permute-done((bf16[8192,128]{1,0:T(8,128)(2,1)S(1)}, bf16[8192,128]{1,0:T(8,128)(2,1)S(1)}, u32[]{:S(2)}, u32[]{:S(2)}) %collective-permute-start.2) | collective-permute-done | bytes 2097184 | tf_op jit(solution)/shard_map/ppermute | solution.py:14
  67.2 25.6 %collective-permute-done.3 = bf16[8192,128]{1,0:T(8,128)(2,1)} collective-permute-done((bf16[8192,128]{1,0:T(8,128)(2,1)S(1)}, bf16[8192,128]{1,0:T(8,128)(2,1)}, u32[]{:S(2)}, u32[]{:S(2)}) %collective-permute-start.3) | collective-permute-done | bytes 2097184 | tf_op jit(solution)/shard_map/ppermute | solution.py:14
  92.7 25.8 %collective-permute-done.4 = bf16[8192,128]{1,0:T(8,128)(2,1)} collective-permute-done((bf16[8192,128]{1,0:T(8,128)(2,1)}, bf16[8192,128]{1,0:T(8,128)(2,1)}, u32[]{:S(2)}, u32[]{:S(2)}) %collective-permute-start.4) | collective-permute-done | bytes 2097184 | tf_op jit(solution)/shard_map/ppermute | solution.py:14
  137.7 11.6 %fusion.1 = f32[512,512]{0,1:T(8,128)} fusion(bf16[8192,1024]{1,0:T(8,128)(2,1)} %constant_dynamic-update-slice_fusion, s32[]{:T(128)S(6)} %select_n.21), kind=kOutput, calls=%fused_computation.4 | convolution fusion | flops 4294967296 | bytes 9437188 | tf_op jit(solution)/shard_map/dot_general | solution.py:39
  150.4 79.0 %all-reduce.4.cloned.1.call-done = f32[512,512]{0,1:T(8,128)} async-done(((f32[512,512]{0,1:T(8,128)}), f32[512,512]{0,1:T(8,128)}) %all-reduce.4.cloned.1.call-update) | async-done | bytes 1048592 | tf_op jit(solution)/shard_map/psum | solution.py:78
  232.5 11.7 %cholesky.104 = f32[128,128]{1,0:T(8,128)S(1)} custom-call(f32[128,128]{1,0:T(8,128)S(1)} %cholesky.266), custom_call_target="Cholesky" | custom-call | tf_op jit(solution)/shard_map/jit(cholesky)/cholesky | solution.py:62
  244.4 9.8 %custom-call.30 = f32[1,128,128]{1,2,0:T(8,128)S(1)} custom-call(f32[1,128,128]{2,1,0:T(8,128)S(1)} %get-tuple-element.37), custom_call_target="InvertDiagBlocksLowerTriangular" | custom-call | tf_op jit(solution)/shard_map/jit(cholesky)/cholesky | solution.py:62
  254.9 11.7 %cholesky.217 = f32[128,128]{1,0:T(8,128)S(1)} custom-call(f32[128,128]{1,0:T(8,128)S(1)} %cholesky.270), custom_call_target="Cholesky" | custom-call | tf_op jit(solution)/shard_map/jit(cholesky)/cholesky | solution.py:62
  266.6 10.0 %custom-call.31 = f32[1,128,128]{1,2,0:T(8,128)S(1)} custom-call(f32[1,128,128]{2,1,0:T(8,128)S(1)} %get-tuple-element.34), custom_call_target="InvertDiagBlocksLowerTriangular" | custom-call | tf_op jit(solution)/shard_map/jit(cholesky)/cholesky | solution.py:62
  277.3 11.7 %cholesky.238 = f32[128,128]{1,0:T(8,128)S(1)} custom-call(f32[128,128]{1,0:T(8,128)S(1)} %cholesky.275), custom_call_target="Cholesky" | custom-call | tf_op jit(solution)/shard_map/jit(cholesky)/cholesky | solution.py:62
  289.0 9.8 %custom-call.32 = f32[1,128,128]{1,2,0:T(8,128)S(1)} custom-call(f32[1,128,128]{2,1,0:T(8,128)S(1)} %get-tuple-element.31), custom_call_target="InvertDiagBlocksLowerTriangular" | custom-call | tf_op jit(solution)/shard_map/jit(cholesky)/cholesky | solution.py:62
  299.4 11.7 %cholesky.255 = f32[128,128]{1,0:T(8,128)S(1)} custom-call(f32[128,128]{1,0:T(8,128)S(1)} %convolution_subtract_fusion.5), custom_call_target="Cholesky" | custom-call | tf_op jit(solution)/shard_map/jit(cholesky)/cholesky | solution.py:62
  316.1 10.1 %while.1 = (s32[]{:T(128)}, f32[512,512]{1,0:T(8,128)S(1)}, s32[4,2]{0,1:T(2,128)S(1)}, f32[4,128,128]{2,1,0:T(8,128)}, s32[]{:T(128)}) while((s32[]{:T(128)}, f32[512,512]{1,0:T(8,128)S(1)}, s32[4,2]{0,1:T(2,128)S(1)}, f32[4,128,128]{2,1,0:T(8,128)}, s32[]{:T(128)}) %tuple.38), condition=%wide.while_cond, body=%wide.while_body.sunk | while | flops 2 | bytes 132205 | solution.py:64
  326.2 40.1 %custom-call.33 = f32[4,128,128]{1,2,0:T(8,128)S(1)} custom-call(f32[4,128,128]{2,1,0:T(8,128)} %get-tuple-element.9), custom_call_target="InvertDiagBlocksLowerTriangular" | custom-call | tf_op jit(solution)/shard_map/triangular_solve | solution.py:64
  370.2 8.8 %convolution_convert_fusion = bf16[8192,512]{1,0:T(8,128)(2,1)S(1)} fusion(bf16[8192,1024]{1,0:T(8,128)(2,1)} %constant_dynamic-update-slice_fusion, s32[]{:T(128)S(6)} %select_n.21, bf16[128,512]{1,0:T(8,128)(2,1)S(1)} %convolution_convert_fusion.1, bf16[128,512]{1,0:T(8,128)(2,1)S(1)} %get-tuple-element.40, bf16[128,512]{1,0:T(8,128)(2,1)S(1)} %get-tuple-element.42, ...), kind=kOutput, calls=%fused_computation.2 | convolution fusion | flops 4301258752 | bytes 17301508 | tf_op jit(solution)/shard_map/dot_general | solution.py:81
  379.4 3.6 collective-permute-start.5
  390.3 3.5 fusion.56
  393.7 10.1 %convert_bitcast_fusion = bf16[32,256,128]{1,2,0:T(8,128)(2,1)} fusion(bf16[32,256,256]{2,1,0:T(8,128)(2,1)} %param.9, f32[32,128,256]{2,1,0:T(8,128)} %fusion.56, f32[32,128,256]{2,1,0:T(8,128)} %fusion.55, bf16[32,256,128]{2,1,0:T(8,128)(2,1)S(1)} %bitcast.100, bf16[32,256,256]{2,1,0:T(8,128)(2,1)} %param.6), kind=kOutput, calls=%fused_computation.16 | convolution fusion | flops 1077936128 | bytes 20971520 | tf_op jit(solution)/shard_map/bij,bjc->bic/dot_general | solution.py:57
  407.1 6.4 %fusion.57 = f32[512,128]{1,0:T(8,128)} fusion(bf16[8192,512]{1,0:T(8,128)(2,1)} %copy-done.7, bf16[8192,128]{1,0:T(8,128)(2,1)S(1)} %bitcast.103), kind=kOutput, calls=%fused_computation.113 | convolution fusion | flops 1073741824 | bytes 10747904 | tf_op jit(solution)/shard_map/dot_general | solution.py:39
  413.5 72.2 %all-reduce.6.cloned.1.call-done = f32[512,128]{1,0:T(8,128)} async-done(((f32[512,128]{1,0:T(8,128)}), f32[512,128]{1,0:T(8,128)}) %all-reduce.6.cloned.1.call-update) | async-done | bytes 262160 | tf_op jit(solution)/shard_map/psum | solution.py:84
  (90 shorter events, 63.2 us)
Async XLA Ops:
  7.2 222.3 %all-reduce.4.cloned.1.call-start = ((), (), s32[]{:S(2)}) async-start(), calls=%async_computation | async-start | bytes 2097152 | tf_op jit(solution)/shard_map/psum | solution.py:78
  8.1 13.3 %collective-permute-start.1 = (bf16[256,128]{1,0:T(8,128)(2,1)S(1)}, bf16[256,128]{1,0:T(8,128)(2,1)S(1)}, u32[]{:S(2)}, u32[]{:S(2)}) collective-permute-start(bf16[256,128]{1,0:T(8,128)(2,1)S(1)} %get-tuple-element.26), channel_id=1, source_target_pairs={{4,0},{8,4},{12,8},{16,12},{20,16},{24,20},{28,24},{5,1},{9,5},{13... | collective-permute-start | bytes 196616 | tf_op jit(solution)/shard_map/ppermute | solution.py:33
  9.4 12.0 %collective-permute-start = (bf16[256,128]{1,0:T(8,128)(2,1)S(1)}, bf16[256,128]{1,0:T(8,128)(2,1)S(1)}, u32[]{:S(2)}, u32[]{:S(2)}) collective-permute-start(bf16[256,128]{1,0:T(8,128)(2,1)S(1)} %get-tuple-element.27), channel_id=1, source_target_pairs={{0,4},{4,8},{8,12},{12,16},{16,20},{20,24},{24,28},{1,5},{5,9},{9,... | collective-permute-start | bytes 196616 | tf_op jit(solution)/shard_map/ppermute | solution.py:30
  14.9 6.5 %copy-start.4 = (bf16[8192,128]{1,0:T(8,128)(2,1)S(1)}, bf16[8192,128]{1,0:T(8,128)(2,1)}, u32[]{:S(2)}) copy-start(bf16[8192,128]{1,0:T(8,128)(2,1)} %param.5) | copy-start | bytes 6291460
  21.4 2.2 copy-start.2
  40.3 25.5 %collective-permute-start.2 = (bf16[8192,128]{1,0:T(8,128)(2,1)S(1)}, bf16[8192,128]{1,0:T(8,128)(2,1)S(1)}, u32[]{:S(2)}, u32[]{:S(2)}) collective-permute-start(bf16[8192,128]{1,0:T(8,128)(2,1)S(1)} %bitcast.95), channel_id=1, source_target_pairs={{0,1},{1,2},{2,3},{3,0},{4,5},{5,6},{6,7},{7,4},{8,9},{9,10},{10,1... | collective-permute-start | bytes 6291464 | tf_op jit(solution)/shard_map/ppermute | solution.py:14
  65.9 1.3 copy-start.5
  67.2 25.6 %collective-permute-start.3 = (bf16[8192,128]{1,0:T(8,128)(2,1)S(1)}, bf16[8192,128]{1,0:T(8,128)(2,1)}, u32[]{:S(2)}, u32[]{:S(2)}) collective-permute-start(bf16[8192,128]{1,0:T(8,128)(2,1)S(1)} %collective-permute-done.2), channel_id=1, source_target_pairs={{0,1},{1,2},{2,3},{3,0},{4,5},{5,6},{6,7},{7,4},{8,9},{9,10},{10,1... | collective-permute-start | bytes 6291464 | tf_op jit(solution)/shard_map/ppermute | solution.py:14
  92.7 25.8 %collective-permute-start.4 = (bf16[8192,128]{1,0:T(8,128)(2,1)}, bf16[8192,128]{1,0:T(8,128)(2,1)}, u32[]{:S(2)}, u32[]{:S(2)}) collective-permute-start(bf16[8192,128]{1,0:T(8,128)(2,1)} %collective-permute-done.3), channel_id=1, source_target_pairs={{0,1},{1,2},{2,3},{3,0},{4,5},{5,6},{6,7},{7,4},{8,9},{9,10},{10,1... | collective-permute-start | bytes 6291464 | tf_op jit(solution)/shard_map/ppermute | solution.py:14
  92.7 32.2 %copy-start.6 = (bf16[8192,128]{1,0:T(8,128)(2,1)S(1)}, bf16[8192,128]{1,0:T(8,128)(2,1)}, u32[]{:S(2)}) copy-start(bf16[8192,128]{1,0:T(8,128)(2,1)} %copy-done.5) | copy-start | bytes 6291460
  149.3 336.5 %all-reduce.6.cloned.1.call-start = ((), (), s32[]{:S(2)}) async-start(), calls=%async_computation.1 | async-start | bytes 524288 | tf_op jit(solution)/shard_map/psum | solution.py:84
  379.0 9.0 %copy-start.7 = (bf16[8192,512]{1,0:T(8,128)(2,1)}, bf16[8192,512]{1,0:T(8,128)(2,1)S(1)}, u32[]{:S(2)}) copy-start(bf16[8192,512]{1,0:T(8,128)(2,1)S(1)} %convolution_convert_fusion) | copy-start | bytes 25165828
  379.1 5.6 %copy-start.3 = (bf16[32,256,256]{2,1,0:T(8,128)(2,1)S(1)}, bf16[32,256,256]{2,1,0:T(8,128)(2,1)}, u32[]{:S(2)}) copy-start(bf16[32,256,256]{2,1,0:T(8,128)(2,1)} %param.7) | copy-start | bytes 12582916
  379.4 9.9 %copy-start = (bf16[8192,128]{1,0:T(8,128)(2,1)}, bf16[8192,128]{1,0:T(8,128)(2,1)S(1)}, u32[]{:S(2)}) copy-start(bf16[8192,128]{1,0:T(8,128)(2,1)S(1)} %constant_dynamic-slice_fusion.2) | copy-start | bytes 6291460
  379.4 8.7 %collective-permute-start.5 = (bf16[256,128]{1,0:T(8,128)(2,1)S(1)}, bf16[256,128]{1,0:T(8,128)(2,1)S(1)}, u32[]{:S(2)}, u32[]{:S(2)}) collective-permute-start(bf16[256,128]{1,0:T(8,128)(2,1)S(1)} %get-tuple-element.20), channel_id=1, source_target_pairs={{0,4},{4,8},{8,12},{12,16},{16,20},{20,24},{24,28},{1,5},{5,9},{9,... | collective-permute-start | bytes 196616 | tf_op jit(solution)/shard_map/ppermute | solution.py:30
  383.0 6.3 %collective-permute-start.6 = (bf16[256,128]{1,0:T(8,128)(2,1)S(1)}, bf16[256,128]{1,0:T(8,128)(2,1)S(1)}, u32[]{:S(2)}, u32[]{:S(2)}) collective-permute-start(bf16[256,128]{1,0:T(8,128)(2,1)S(1)} %get-tuple-element.21), channel_id=1, source_target_pairs={{4,0},{8,4},{12,8},{16,12},{20,16},{24,20},{28,24},{5,1},{9,5},{13... | collective-permute-start | bytes 196616 | tf_op jit(solution)/shard_map/ppermute | solution.py:33
  388.1 2.2 copy-start.1
Sparse Core Ops, SparseCore 0:
  149.4 79.9 all-reduce.3
  413.7 72.0 all-reduce.5
